TPU v7x, 16 devices: a whole 2x2x2 slice. The times are simulated.
16 devices in a mesh: dep: 2 (over z), col: 2 (over y), row: 4 (over x, core).
Axes of the slice: x: 2, y: 2, z: 2, core: 2. Of those that a mesh axis runs over, the one named last changes fastest.
Arguments:
- a_mat: bfloat16 [12288, 12288], P('row', 'col')
- b_mat: bfloat16 [12288, 12288], P('row', 'col')
Outputs:
- output: float32 [12288, 12288], P('row', ('col', 'dep'))
All inputs are finite; a program needn't handle non-finite values.
Results may differ from a plain program's by a relative error of at most 0.001.
Values are sent between devices in bfloat16 or wider.
A program may use at most 1 GiB of HBM per device.

v0:
```python
import jax
import jax.numpy as jnp
from jax import lax
from jax.sharding import PartitionSpec as P


def solution(mesh):
    n_dep = mesh.shape['dep']
    n_row = mesh.shape['row']
    n_col = mesh.shape['col']

    def local_product(a_blk, b_blk):
        layer_idx = lax.axis_index('dep')
        rows_a, cols_a = a_blk.shape
        cols_b = b_blk.shape[1]
        unit_len = cols_a // (n_row * n_dep)
        a_part = a_blk.reshape(rows_a, n_row, n_dep, unit_len)
        a_part = lax.dynamic_index_in_dim(a_part, layer_idx, axis=2, keepdims=False)
        a_part = a_part.reshape(rows_a, n_row * unit_len)
        b_part = b_blk.reshape(n_col, n_dep, unit_len, cols_b)
        b_part = lax.dynamic_index_in_dim(b_part, layer_idx, axis=1, keepdims=False)
        b_part = b_part.reshape(n_col * unit_len, cols_b)
        a_panel = lax.all_gather(a_part, 'col', axis=1, tiled=True)
        b_panel = lax.all_gather(b_part, 'row', axis=0, tiled=True)
        part_sum = jnp.dot(a_panel, b_panel, preferred_element_type=jnp.float32)
        return lax.psum_scatter(part_sum, 'dep', scatter_dimension=1, tiled=True)

    return jax.shard_map(local_product, mesh=mesh, in_specs=(P('row', 'col'), P('row', 'col')), out_specs=P('row', ('col', 'dep')), check_vma=False)
```

profile of v0, /device:TPU:0, one launch (start us, length us, event | category | flops | bytes accessed | tf_op | source)
XLA Modules:
  0.0 2023.7 jit_solution(2415218552408225548)
XLA Ops:
  6.5 0.0 all-gather.3.cloned.1.call-start
  6.5 48.5 %copy.3 = bf16[3072,6144]{0,1:T(8,128)(2,1)} copy(bf16[3072,6144]{1,0:T(8,128)(2,1)} %param.2) | data formatting | bytes 75497472 | tf_op args[0]
  55.1 16.8 constant_dynamic-slice_fusion.1
  71.9 0.0 all-gather.3.cloned.1.call-update
  71.9 0.0 all-gather.5.cloned.1.call-start
  71.9 17.0 constant_dynamic-slice_fusion
  88.9 0.0 all-gather.5.cloned.1.call-update
  88.9 0.0 reduce-scatter.2.cloned.1.call-start
  89.0 420.6 %all-gather.3.cloned.1.call-done = bf16[3072,6144]{0,1:T(8,128)(2,1)} async-done(((bf16[3072,3072]{0,1:T(8,128)(2,1)}), bf16[3072,6144]{0,1:T(8,128)(2,1)}) %all-gather.3.cloned.1.call-update) | async-done | bytes 37748752 | tf_op jit(solution)/shard_map/all_gather | solution.py:23
  509.6 440.8 %all-gather.5.cloned.1.call-done = bf16[6144,6144]{1,0:T(8,128)(2,1)} async-done(((bf16[1536,6144]{1,0:T(8,128)(2,1)}), bf16[6144,6144]{1,0:T(8,128)(2,1)}) %all-gather.5.cloned.1.call-update) | async-done | bytes 75497488 | tf_op jit(solution)/shard_map/all_gather | solution.py:24
  950.4 250.1 %fusion = f32[3072,6144]{1,0:T(8,128)} fusion(bf16[3072,6144]{0,1:T(8,128)(2,1)} %all-gather.3.cloned.1.call-done, bf16[6144,6144]{1,0:T(8,128)(2,1)} %all-gather.5.cloned.1.call-done), kind=kOutput, calls=%fused_computation.2 | convolution fusion | flops 231928233984 | bytes 188743680 | tf_op jit(solution)/shard_map/dot_general | solution.py:25
  1200.5 0.0 reduce-scatter.2.cloned.1.call-update
  1200.6 816.7 %reduce-scatter.2.cloned.1.call-done = f32[3072,3072]{1,0:T(8,128)} async-done(((f32[3072,6144]{1,0:T(8,128)}), f32[3072,3072]{1,0:T(8,128)}) %reduce-scatter.2.cloned.1.call-update) | async-done | bytes 37748752 | tf_op jit(solution)/shard_map/reduce_scatter | solution.py:26
Async XLA Ops:
  6.5 503.0 %all-gather.3.cloned.1.call-start = ((), (), s32[]{:S(2)}) async-start(), calls=%async_computation.1 | async-start | bytes 56623104 | tf_op jit(solution)/shard_map/all_gather | solution.py:23
  71.9 878.5 %all-gather.5.cloned.1.call-start = ((), (), s32[]{:S(2)}) async-start(), calls=%async_computation.2 | async-start | bytes 94371840 | tf_op jit(solution)/shard_map/all_gather | solution.py:24
  88.9 1928.3 %reduce-scatter.2.cloned.1.call-start = ((), (), s32[]{:S(2)}) async-start(), calls=%async_computation.3 | async-start | bytes 113246208 | tf_op jit(solution)/shard_map/reduce_scatter | solution.py:26
Sparse Core Ops, SparseCore 0:
  72.0 437.5 all-gather.2
  511.1 439.2 all-gather.4
  1200.7 816.4 reduce-scatter.1
where the time goes:
time: 2030 us; the launch traced here: 2020 us
  waiting for transfers between devices  1680 us (83%)
  matrix products  250 us (12%)
  local copies, waits for them, and re-layouts  82.3 us (4%)
    reduce_scatter x1, waiting for transfers between devices, local_product(): return lax.psum_scatter(part_sum, 'dep', scatter_dimension=1, tiled=True)  817 us
    all_gather x1, waiting for transfers between devices, local_product(): b_panel = lax.all_gather(b_part, 'row', axis=0, tiled=True)  441 us
    all_gather x1, waiting for transfers between devices, local_product(): a_panel = lax.all_gather(a_part, 'col', axis=1, tiled=True)  421 us
    dot_general x1, matrix products, local_product(): part_sum = jnp.dot(a_panel, b_panel, preferred_element_type=jnp.float32)  250 us
    unnamed x1, local copies, waits for them, and re-layouts  48.5 us
  transfers between devices with their start and end apart: 3, of which 3 were waited for; matrix products, arithmetic and copies ran while one was open for 1% of the time, Pallas kernels for 0%

commit v1 on v0

v1 whole, which is shorter than its diff:
```python
import functools

import jax
import jax.numpy as jnp
from jax import lax
from jax.experimental import pallas as pl
from jax.experimental.pallas import tpu as pltpu
from jax.sharding import PartitionSpec as P

MESH = pl.DeviceIdType.MESH
KC = 128
Q = 3
YD = 4
ZD = 4
TILES = 6
XD = 2


def gather_kernel(
    a_ref, b_ref,
    c_ref, abuf, bbuf, ay, az, bx, bp, bq,
    ysend, yrecv, zsend, zrecv, xsend, xrecv, psend, precv, qsend, qrecv, ldsem,
):
    z, y, i = lax.axis_index("dep"), lax.axis_index("col"), lax.axis_index("row")
    m = a_ref.shape[0]
    mq, tn = m // Q, m // TILES
    rounds = m // KC
    ticks = rounds * Q
    z_to, y_to = {"dep": 1 - z}, {"col": 1 - y}
    x_to, p_to = {"row": lax.rem(i + 2, 4)}, {"row": i + 1 - 2 * lax.rem(i, 2)}

    def y_copy(s):
        t, rows = s // Q, pl.ds(pl.multiple_of(lax.rem(s, Q) * mq, mq), mq)
        cols = pl.ds(pl.multiple_of(z * m + t * KC, KC), KC)
        return pltpu.make_async_remote_copy(
            a_ref.at[rows, cols], ay.at[t, rows, :], ysend.at[lax.rem(s, YD)], yrecv.at[s],
            device_id=y_to, device_id_type=MESH,
        )

    def z_copy(s):
        t, rows = s // Q, pl.ds(pl.multiple_of(lax.rem(s, Q) * mq, mq), mq)
        return pltpu.make_async_remote_copy(
            ay.at[t, rows, :], az.at[t, rows, :], zsend.at[lax.rem(s, ZD)], zrecv.at[s],
            device_id=z_to, device_id_type=MESH,
        )

    def b_rows(t):
        return pl.ds(pl.multiple_of(t * KC, KC), KC)

    def b_piece(t):
        return b_ref.at[b_rows(t), pl.ds(pl.multiple_of(z * m, m), m)]

    def x_copy(t):
        return pltpu.make_async_remote_copy(
            b_piece(t), bx.at[b_rows(t), :], xsend.at[lax.rem(t, XD)], xrecv.at[t],
            device_id=x_to, device_id_type=MESH,
        )

    def p_copy(t):
        return pltpu.make_async_remote_copy(
            b_piece(t), bp.at[b_rows(t), :], psend.at[lax.rem(t, XD)], precv.at[t],
            device_id=p_to, device_id_type=MESH,
        )

    def q_copy(t):
        return pltpu.make_async_remote_copy(
            bx.at[b_rows(t), :], bq.at[b_rows(t), :], qsend.at[lax.rem(t, XD)], qrecv.at[t],
            device_id=p_to, device_id_type=MESH,
        )

    def place(k):
        far = 2 + jnp.where(lax.rem(k, 2) == z, 0, 1)
        return jnp.where(k // 2 == y, lax.rem(k, 2), far)

    def loads(t, slot):
        swap = 1 - 2 * lax.rem(i, 2)
        far = lax.rem(i + 2, 4)

        def a_dst(p):
            return abuf.at[slot, :, pl.ds(p * KC, KC)]

        def b_dst(k):
            return bbuf.at[slot, pl.ds(pl.multiple_of(place(k) * KC, KC), KC), :]

        def a_src(h):
            return a_ref.at[:, pl.ds(pl.multiple_of(h * m + t * KC, KC), KC)]

        pairs = [
            (a_src(0), a_dst(0)),
            (a_src(1), a_dst(1)),
            (ay.at[t], a_dst(2)),
            (b_piece(t), b_dst(i)),
            (bp.at[b_rows(t), :], b_dst(i + swap)),
            (bx.at[b_rows(t), :], b_dst(far)),
            (bq.at[b_rows(t), :], b_dst(far + swap)),
            (az.at[t], a_dst(3)),
        ]
        return [pltpu.make_async_copy(s, d, ldsem.at[slot, n]) for n, (s, d) in enumerate(pairs)]

    def compute(q, slot):
        rows = pl.ds(pl.multiple_of(q * mq, mq), mq)

        @pl.loop(0, m // tn)
        def _(n):
            cols = pl.ds(pl.multiple_of(n * tn, tn), tn)
            c_ref[rows, cols] += jnp.dot(
                abuf[slot, rows, :], bbuf[slot, :, cols], preferred_element_type=jnp.float32
            )

    barrier = pltpu.get_barrier_semaphore()
    for to in (z_to, y_to, x_to, p_to):
        pl.semaphore_signal(barrier, inc=1, device_id=to, device_id_type=MESH)
    pl.semaphore_wait(barrier, 4)

    for s in range(YD):
        y_copy(s).start()
    for t in range(XD):
        x_copy(t).start()
        p_copy(t).start()

    @pl.loop(0, m // 128)
    def _(n):
        rows = pl.ds(pl.multiple_of(n * 128, 128), 128)
        c_ref[rows, :] = jnp.zeros((128, m), jnp.float32)

    @pl.loop(0, ticks)
    def _(s):
        r, q = s // Q, lax.rem(s, Q)

        @pl.when(s >= ZD)
        def _():
            z_copy(s - ZD).wait_send()

        y_copy(s).wait_recv()
        z_copy(s).start()
        y_copy(s).wait_send()

        @pl.when(s + YD < ticks)
        def _():
            y_copy(s + YD).start()

        @pl.when((q == 1) & (r >= 1))
        def _():
            for k in range(Q):
                z_copy((r - 1) * Q + k).wait_recv()
            p_copy(r - 1).wait_recv()
            q_copy(r - 1).wait_recv()
            for ld in loads(r - 1, lax.rem(r - 1, 2)):
                ld.start()

        @pl.when(q == Q - 1)
        def _():
            @pl.when(r >= XD)
            def _():
                q_copy(r - XD).wait_send()

            x_copy(r).wait_recv()
            q_copy(r).start()
            x_copy(r).wait_send()
            p_copy(r).wait_send()

            @pl.when(r + XD < rounds)
            def _():
                x_copy(r + XD).start()
                p_copy(r + XD).start()

        @pl.when(r >= 2)
        def _():
            slot = lax.rem(r, 2)

            @pl.when(q == 0)
            def _():
                for ld in loads(r - 2, slot):
                    ld.wait()

            compute(q, slot)

    last = rounds - 1
    final = loads(last, last % 2)
    p_copy(last).wait_recv()
    for ld in final[:6]:
        ld.start()
    q_copy(last).wait_recv()
    final[6].start()
    for ld in loads(last - 1, (last - 1) % 2):
        ld.wait()

    @pl.loop(0, Q)
    def _(q):
        compute(q, (last - 1) % 2)

    for k in range(Q):
        z_copy(last * Q + k).wait_recv()
    final[7].start()
    for s in range(ticks - ZD, ticks):
        z_copy(s).wait_send()
    for t in range(rounds - XD, rounds):
        q_copy(t).wait_send()
    for ld in final:
        ld.wait()


def finish_kernel(slot, c_ref, abuf, bbuf, out, stage, sem):
    m = c_ref.shape[0]
    slots, tm, tn = stage.shape
    across = m // tn
    tiles = (m // tm) * across

    def spot(n):
        return pl.ds(pl.multiple_of(n // across * tm, tm), tm), pl.ds(pl.multiple_of(lax.rem(n, across) * tn, tn), tn)

    def write(n):
        at = lax.rem(n, slots)
        rows, cols = spot(n)
        return pltpu.make_async_copy(stage.at[at], out.at[rows, cols], sem.at[at])

    @pl.loop(0, tiles)
    def _(n):
        rows, cols = spot(n)

        @pl.when(n >= slots)
        def _():
            write(n - slots).wait()

        stage[lax.rem(n, slots)] = c_ref[rows, cols] + jnp.dot(
            abuf[slot, rows, :], bbuf[slot, :, cols], preferred_element_type=jnp.float32
        )
        write(n).start()

    for n in range(tiles - slots, tiles):
        write(n).wait()


def solution(mesh):
    def local_product(a_blk, b_blk):
        m = a_blk.shape[0]
        rounds = m // KC
        ticks = rounds * Q
        any_spec = pl.BlockSpec(memory_space=pl.ANY)
        vmem_spec = pl.BlockSpec(memory_space=pltpu.VMEM)
        dma = pltpu.SemaphoreType.DMA
        c, abuf, bbuf, *_ = pl.pallas_call(
            gather_kernel,
            name="gather",
            out_shape=(
                pltpu.VMEM((m, m), jnp.float32),
                pltpu.VMEM((2, m, 4 * KC), jnp.bfloat16),
                pltpu.VMEM((2, 4 * KC, m), jnp.bfloat16),
                pltpu.HBM((rounds, m, KC), jnp.bfloat16),
                pltpu.HBM((rounds, m, KC), jnp.bfloat16),
                pltpu.HBM((m, m), jnp.bfloat16),
                pltpu.HBM((m, m), jnp.bfloat16),
                pltpu.HBM((m, m), jnp.bfloat16),
            ),
            in_specs=[any_spec] * 2,
            out_specs=(vmem_spec,) * 3 + (any_spec,) * 5,
            scratch_shapes=[
                dma((YD,)), dma((ticks,)), dma((ZD,)), dma((ticks,)), dma((XD,)), dma((rounds,)),
                dma((XD,)), dma((rounds,)), dma((XD,)), dma((rounds,)), dma((2, 8)),
            ],
            compiler_params=pltpu.CompilerParams(
                collective_id=0, has_side_effects=True, vmem_limit_bytes=4 * 2**20
            ),
        )(a_blk, b_blk)
        c, abuf, bbuf = (pltpu.with_memory_space_constraint(v, pltpu.VMEM) for v in (c, abuf, bbuf))
        tm, tn = m // 12, m // 6
        return pl.pallas_call(
            functools.partial(finish_kernel, (rounds - 1) % 2),
            name="finish",
            out_shape=jax.ShapeDtypeStruct((m, m), jnp.float32),
            in_specs=[vmem_spec] * 3,
            out_specs=any_spec,
            scratch_shapes=[pltpu.VMEM((5, tm, tn), jnp.float32), dma((5,))],
            compiler_params=pltpu.CompilerParams(vmem_limit_bytes=4 * 2**20),
        )(c, abuf, bbuf)

    return jax.shard_map(
        local_product, mesh=mesh, in_specs=(P("row", "col"), P("row", "col")), out_specs=P("row", ("col", "dep")), check_vma=False
    )
```

time: 2030 us -> 454 us (0.22)
  waiting for transfers between devices: 1680 us -> 0 us
  Pallas kernels: 0 us -> 454 us
  matrix products: 250 us -> 0 us
  local copies, waits for them, and re-layouts: 82.3 us -> 0 us
    all_gather x2 -> x0, waiting for transfers between devices: 861 us -> none  [the longest x1 441 us: local_product(): b_panel = lax.all_gather(b_part, 'row', axis=0, tiled=True)]
    reduce_scatter x1 -> x0, waiting for transfers between devices: 817 us -> none  [local_product(): return lax.psum_scatter(part_sum, 'dep', scatter_dimension=1, tiled=True)]
    pallas_call x0 -> x2, Pallas kernels: none -> 454 us  [the longest x1 430 us: local_product(): pl.pallas_call(gather_kernel, name='gather', out_shape=(pltpu.VMEM((m, m)...]
    dot_general x1 -> x0, matrix products: 250 us -> none  [local_product(): part_sum = jnp.dot(a_panel, b_panel, preferred_element_type=jnp.float32)]
    unnamed x1 -> x0, local copies, waits for them, and re-layouts: 48.5 us -> none
    dynamic_slice x2 -> x0, local copies, waits for them, and re-layouts: 33.8 us -> none  [the longest x1 17 us: local_product(): b_part = lax.dynamic_index_in_dim(b_part, layer_idx, axis=1, keepdims=False)]
  transfers between devices with their start and end apart: 3 -> 0, of which waited for: 3 -> 0; matrix products, arithmetic and copies ran while one was open for 1% -> 0% of each run, Pallas kernels for 0% -> 0%
where the time goes in v1:
time: 454 us
  Pallas kernels  454 us (100%)
    pallas_call x1, Pallas kernels, local_product(): pl.pallas_call(gather_kernel, name='gather', out_shape=(pltpu.VMEM((m, m)...  430 us
    pallas_call x1, Pallas kernels, local_product(): pl.pallas_call(functools.partial(finish_kernel, (rounds - 1) % 2), name='...  23.4 us

profile of v1, /device:TPU:0, one launch (start us, length us, event | category | flops | bytes accessed | tf_op | source)
XLA Modules:
  0.0 453.6 jit_solution(1668798230302874512)
XLA Ops:
  0.0 430.2 %gather.1 = (f32[3072,3072]{1,0:T(8,128)S(1)}, bf16[2,3072,512]{2,1,0:T(8,128)(2,1)S(1)}, bf16[2,512,3072]{2,1,0:T(8,128)(2,1)S(1)}, bf16[24,3072,128]{2,1,0:T(8...) custom-call(bf16[3072,6144]{1,0:T(8,128)(2,1)} %a_ref.1, ...), custom_call_target="tpu_custom_call" | custom-call | tf_op jit(solution)/shard_map/gather/pallas_call | solution.py:242
  430.2 23.4 %finish.1 = f32[3072,3072]{1,0:T(8,128)} custom-call(f32[3072,3072]{1,0:T(8,128)S(1)} %get-tuple-element.8.c_ref, bf16[2,3072,512]{2,1,0:T(8,128)(2,1)S(1)} %get-tuple-element.9.abuf, bf16[2,512,3072]{2,1,0:T(8,128)(2,1)S(1)} %get-tuple-element.10.bbuf), custom_call_target="tpu_custom_call" | custom-call | tf_op jit(solution)/shard_map/finish/pallas_call | solution.py:267

commit v2 on v1

v2 whole, which is shorter than its diff:
```python
import functools

import jax
import jax.numpy as jnp
from jax import lax
from jax.experimental import pallas as pl
from jax.experimental.pallas import tpu as pltpu
from jax.sharding import PartitionSpec as P

MESH = pl.DeviceIdType.MESH
KC = 128
Q = 6
NT = 3
YD = 6
ZD = 6
XD = 2
LOAD = 4
AHEAD = 3
WORK = Q + 2


def gather_kernel(
    a_ref, b_ref,
    c_ref, abuf, bbuf, ay, az, bx, bp, bq,
    ysend, yrecv, zsend, zrecv, xsend, xrecv, psend, precv, qsend, qrecv, asem, bsem,
):
    z, y, i = lax.axis_index("dep"), lax.axis_index("col"), lax.axis_index("row")
    m = a_ref.shape[0]
    mq, tn = m // Q, m // NT
    rounds = m // KC
    ticks = rounds * Q
    z_to, y_to = {"dep": 1 - z}, {"col": 1 - y}
    swap = 1 - 2 * lax.rem(i, 2)
    far = lax.rem(i + 2, 4)
    x_to, p_to = {"row": far}, {"row": i + swap}

    def a_rows(s):
        return pl.ds(pl.multiple_of(lax.rem(s, Q) * mq, mq), mq)

    def a_piece(s, h):
        return a_ref.at[a_rows(s), pl.ds(pl.multiple_of(h * m + s // Q * KC, KC), KC)]

    def b_rows(t):
        return pl.ds(pl.multiple_of(t * KC, KC), KC)

    def b_piece(t):
        return b_ref.at[b_rows(t), pl.ds(pl.multiple_of(z * m, m), m)]

    def y_copy(s):
        return pltpu.make_async_remote_copy(
            a_piece(s, z), ay.at[s // Q, a_rows(s), :], ysend.at[lax.rem(s, YD)], yrecv.at[s],
            device_id=y_to, device_id_type=MESH,
        )

    def z_copy(s):
        return pltpu.make_async_remote_copy(
            ay.at[s // Q, a_rows(s), :], az.at[s // Q, a_rows(s), :], zsend.at[lax.rem(s, ZD)], zrecv.at[s],
            device_id=z_to, device_id_type=MESH,
        )

    def x_copy(t):
        return pltpu.make_async_remote_copy(
            b_piece(t), bx.at[b_rows(t), :], xsend.at[lax.rem(t, XD)], xrecv.at[t],
            device_id=x_to, device_id_type=MESH,
        )

    def p_copy(t):
        return pltpu.make_async_remote_copy(
            b_piece(t), bp.at[b_rows(t), :], psend.at[lax.rem(t, XD)], precv.at[t],
            device_id=p_to, device_id_type=MESH,
        )

    def q_copy(t):
        return pltpu.make_async_remote_copy(
            bx.at[b_rows(t), :], bq.at[b_rows(t), :], qsend.at[lax.rem(t, XD)], qrecv.at[t],
            device_id=p_to, device_id_type=MESH,
        )

    def place(k):
        return jnp.where(k // 2 == y, lax.rem(k, 2), 2 + jnp.where(lax.rem(k, 2) == z, 0, 1))

    def a_loads(s):
        slot = lax.rem(s // Q, 2)
        sources = [a_piece(s, 0), a_piece(s, 1), ay.at[s // Q, a_rows(s), :], az.at[s // Q, a_rows(s), :]]
        return [
            pltpu.make_async_copy(
                src, abuf.at[slot, a_rows(s), pl.ds(p * KC, KC)], asem.at[lax.rem(s, AHEAD + Q), p]
            )
            for p, src in enumerate(sources)
        ]

    def b_loads(t):
        slot = lax.rem(t, 2)
        sources = [
            (b_piece(t), i),
            (bp.at[b_rows(t), :], i + swap),
            (bx.at[b_rows(t), :], far),
            (bq.at[b_rows(t), :], far + swap),
        ]
        return [
            pltpu.make_async_copy(
                src, bbuf.at[slot, pl.ds(pl.multiple_of(place(k) * KC, KC), KC), :], bsem.at[slot, n]
            )
            for n, (src, k) in enumerate(sources)
        ]

    def compute(s):
        slot, rows = lax.rem(s // Q, 2), a_rows(s)
        for n in range(NT):
            cols = pl.ds(n * tn, tn)
            c_ref[rows, cols] += jnp.dot(
                abuf[slot, rows, :], bbuf[slot, :, cols], preferred_element_type=jnp.float32
            )

    barrier = pltpu.get_barrier_semaphore()
    for to in (z_to, y_to, x_to, p_to):
        pl.semaphore_signal(barrier, inc=1, device_id=to, device_id_type=MESH)
    pl.semaphore_wait(barrier, 4)

    for s in range(YD):
        y_copy(s).start()
    for t in range(XD):
        x_copy(t).start()
        p_copy(t).start()

    @pl.loop(0, m // 128)
    def _(n):
        rows = pl.ds(pl.multiple_of(n * 128, 128), 128)
        c_ref[rows, :] = jnp.zeros((128, m), jnp.float32)

    def work(s):
        for ld in a_loads(s):
            ld.wait()

        @pl.when(lax.rem(s, Q) == 0)
        def _():
            for ld in b_loads(s // Q):
                ld.wait()

        compute(s)

    def load(s):
        z_copy(s).wait_recv()
        for ld in a_loads(s):
            ld.start()

    @pl.loop(0, ticks + WORK - Q)
    def _(s):
        r, q = s // Q, lax.rem(s, Q)

        @pl.when(s < ticks)
        def _():
            @pl.when(s >= ZD)
            def _():
                z_copy(s - ZD).wait_send()

            y_copy(s).wait_recv()
            z_copy(s).start()
            y_copy(s).wait_send()

            @pl.when(s + YD < ticks)
            def _():
                y_copy(s + YD).start()

            @pl.when(q == Q - 1)
            def _():
                @pl.when(r >= XD)
                def _():
                    q_copy(r - XD).wait_send()

                x_copy(r).wait_recv()
                q_copy(r).start()
                x_copy(r).wait_send()
                p_copy(r).wait_send()

                @pl.when(r + XD < rounds)
                def _():
                    x_copy(r + XD).start()
                    p_copy(r + XD).start()

        @pl.when((q == 1) & (r >= 1))
        def _():
            p_copy(r - 1).wait_recv()
            q_copy(r - 1).wait_recv()
            for ld in b_loads(r - 1):
                ld.start()

        @pl.when((s >= LOAD) & (s - LOAD < ticks))
        def _():
            load(s - LOAD)

        @pl.when(s >= WORK)
        def _():
            work(s - WORK)

    for s in range(ticks + WORK - Q - LOAD, ticks):
        load(s)
    for s in range(ticks - ZD, ticks):
        z_copy(s).wait_send()
    for t in range(rounds - XD, rounds):
        q_copy(t).wait_send()
    for s in range(ticks - Q, ticks):
        for ld in a_loads(s):
            ld.wait()
    for ld in b_loads(rounds - 1):
        ld.wait()


def finish_kernel(slot, c_ref, abuf, bbuf, out, total, sem):
    m = c_ref.shape[0]
    tm, tn = m // Q, m // NT

    def write(k, n):
        at = pl.ds(pl.multiple_of(k * tm, tm), tm), pl.ds(n * tn, tn)
        return pltpu.make_async_copy(total.at[at], out.at[at], sem.at[k, n])

    @pl.loop(0, Q)
    def _(k):
        rows = pl.ds(pl.multiple_of(k * tm, tm), tm)
        for n in range(NT):
            cols = pl.ds(n * tn, tn)
            total[rows, cols] = c_ref[rows, cols] + jnp.dot(
                abuf[slot, rows, :], bbuf[slot, :, cols], preferred_element_type=jnp.float32
            )
            write(k, n).start()

    @pl.loop(0, Q)
    def _(k):
        for n in range(NT):
            write(k, n).wait()


def solution(mesh):
    def local_product(a_blk, b_blk):
        m = a_blk.shape[0]
        rounds = m // KC
        ticks = rounds * Q
        any_spec = pl.BlockSpec(memory_space=pl.ANY)
        vmem_spec = pl.BlockSpec(memory_space=pltpu.VMEM)
        dma = pltpu.SemaphoreType.DMA
        c, abuf, bbuf, *_ = pl.pallas_call(
            gather_kernel,
            name="gather",
            out_shape=(
                pltpu.VMEM((m, m), jnp.float32),
                pltpu.VMEM((2, m, 4 * KC), jnp.bfloat16),
                pltpu.VMEM((2, 4 * KC, m), jnp.bfloat16),
                pltpu.HBM((rounds, m, KC), jnp.bfloat16),
                pltpu.HBM((rounds, m, KC), jnp.bfloat16),
                pltpu.HBM((m, m), jnp.bfloat16),
                pltpu.HBM((m, m), jnp.bfloat16),
                pltpu.HBM((m, m), jnp.bfloat16),
            ),
            in_specs=[any_spec] * 2,
            out_specs=(vmem_spec,) * 3 + (any_spec,) * 5,
            scratch_shapes=[
                dma((YD,)), dma((ticks,)), dma((ZD,)), dma((ticks,)), dma((XD,)), dma((rounds,)),
                dma((XD,)), dma((rounds,)), dma((XD,)), dma((rounds,)), dma((AHEAD + Q, 4)), dma((2, 4)),
            ],
            compiler_params=pltpu.CompilerParams(
                collective_id=0, has_side_effects=True, vmem_limit_bytes=4 * 2**20
            ),
        )(a_blk, b_blk)
        c, abuf, bbuf = (pltpu.with_memory_space_constraint(v, pltpu.VMEM) for v in (c, abuf, bbuf))
        return pl.pallas_call(
            functools.partial(finish_kernel, (rounds - 1) % 2),
            name="finish",
            out_shape=(jax.ShapeDtypeStruct((m, m), jnp.float32), pltpu.VMEM((m, m), jnp.float32)),
            in_specs=[vmem_spec] * 3,
            out_specs=(any_spec, vmem_spec),
            input_output_aliases={0: 1},
            scratch_shapes=[dma((Q, NT))],
            compiler_params=pltpu.CompilerParams(vmem_limit_bytes=4 * 2**20),
        )(c, abuf, bbuf)[0]

    return jax.shard_map(
        local_product, mesh=mesh, in_specs=(P("row", "col"), P("row", "col")), out_specs=P("row", ("col", "dep")), check_vma=False
    )
```

time: 454 us -> 435 us (0.958)
  Pallas kernels: 454 us -> 435 us
    pallas_call x1, Pallas kernels: 430 us -> 421 us  [local_product(): pl.pallas_call(gather_kernel, name='gather', out_shape=(pltpu.VMEM((m, m)...]
    pallas_call x1, Pallas kernels: 23.4 us -> 14.1 us  [local_product(): pl.pallas_call(functools.partial(finish_kernel, (rounds - 1) % 2), name='...]
where the time goes in v2:
time: 435 us
  Pallas kernels  435 us (100%)
    pallas_call x1, Pallas kernels, local_product(): pl.pallas_call(gather_kernel, name='gather', out_shape=(pltpu.VMEM((m, m)...  421 us
    pallas_call x1, Pallas kernels, local_product(): pl.pallas_call(functools.partial(finish_kernel, (rounds - 1) % 2), name='...  14.1 us

profile of v2, /device:TPU:0, one launch (start us, length us, event | category | flops | bytes accessed | tf_op | source)
XLA Modules:
  0.0 434.8 jit_solution(1972904839492836609)
XLA Ops:
  0.0 420.7 %gather.1 = (f32[3072,3072]{1,0:T(8,128)S(1)}, bf16[2,3072,512]{2,1,0:T(8,128)(2,1)S(1)}, bf16[2,512,3072]{2,1,0:T(8,128)(2,1)S(1)}, bf16[24,3072,128]{2,1,0:T(8...) custom-call(bf16[3072,6144]{1,0:T(8,128)(2,1)} %a_ref.1, ...), custom_call_target="tpu_custom_call" | custom-call | tf_op jit(solution)/shard_map/gather/pallas_call | solution.py:241
  420.7 14.1 %finish.1 = (f32[3072,3072]{1,0:T(8,128)}, f32[3072,3072]{1,0:T(8,128)S(1)}) custom-call(f32[3072,3072]{1,0:T(8,128)S(1)} %get-tuple-element.9.c_ref, bf16[2,3072,512]{2,1,0:T(8,128)(2,1)S(1)} %get-tuple-element.10.abuf, bf16[2,512,3072]{2,1,0:T(8,128)(2,1)S(1)} %get-tuple-element.11.bbuf), custom_call_target="tpu_custom_call", output_to_operand_aliasing={{1}: (0, {})} | custom-call | tf_op jit(solution)/shard_map/finish/pallas_call | solution.py:265

commit v3 on v2

--- a/solution.py
+++ b/solution.py
@@ -13,22 +13,25 @@
 NT = 3
 YD = 6
 ZD = 6
-XD = 2
+HALF = KC // 2
+XD = 4
+PD = 2
 LOAD = 4
 AHEAD = 3
-WORK = Q + 2
+WORK = Q + 1
 
 
 def gather_kernel(
     a_ref, b_ref,
     c_ref, abuf, bbuf, ay, az, bx, bp, bq,
-    ysend, yrecv, zsend, zrecv, xsend, xrecv, psend, precv, qsend, qrecv, asem, bsem,
+    ysend, yrecv, zsend, zrecv, wsend, xsend, xrecv, psend, precv, qsend, qrecv, asem, bsem, yfree, zfree, pfree,
 ):
     z, y, i = lax.axis_index("dep"), lax.axis_index("col"), lax.axis_index("row")
     m = a_ref.shape[0]
     mq, tn = m // Q, m // NT
     rounds = m // KC
-    ticks = rounds * Q
+    ticks, halves = rounds * Q, 2 * rounds
+    last_slot = (rounds - 1) % 2
     z_to, y_to = {"dep": 1 - z}, {"col": 1 - y}
     swap = 1 - 2 * lax.rem(i, 2)
     far = lax.rem(i + 2, 4)
@@ -58,38 +61,63 @@
             device_id=z_to, device_id_type=MESH,
         )
 
-    def x_copy(t):
-        return pltpu.make_async_remote_copy(
-            b_piece(t), bx.at[b_rows(t), :], xsend.at[lax.rem(t, XD)], xrecv.at[t],
+    def z_direct(s):
+        return pltpu.make_async_remote_copy(
+            ay.at[s // Q, a_rows(s), :], abuf.at[last_slot, a_rows(s), pl.ds(3 * KC, KC)],
+            zsend.at[lax.rem(s, ZD)], zrecv.at[s],
+            device_id=z_to, device_id_type=MESH,
+        )
+
+    def w_copy():
+        s = ticks - 1
+        return pltpu.make_async_remote_copy(
+            a_piece(s, 1 - z), abuf.at[last_slot, a_rows(s), pl.ds(3 * KC, KC)], wsend, zrecv.at[s],
+            device_id=y_to, device_id_type=MESH,
+        )
+
+    def half_rows(u):
+        return pl.ds(pl.multiple_of(u * HALF, HALF), HALF)
+
+    def x_copy(u):
+        return pltpu.make_async_remote_copy(
+            b_ref.at[half_rows(u), pl.ds(pl.multiple_of(z * m, m), m)], bx.at[half_rows(u), :],
+            xsend.at[lax.rem(u, XD)], xrecv.at[u],
             device_id=x_to, device_id_type=MESH,
         )
 
     def p_copy(t):
         return pltpu.make_async_remote_copy(
-            b_piece(t), bp.at[b_rows(t), :], psend.at[lax.rem(t, XD)], precv.at[t],
+            b_piece(t), bp.at[b_rows(t), :], psend.at[lax.rem(t, PD)], precv.at[t],
             device_id=p_to, device_id_type=MESH,
         )
 
-    def q_copy(t):
-        return pltpu.make_async_remote_copy(
-            bx.at[b_rows(t), :], bq.at[b_rows(t), :], qsend.at[lax.rem(t, XD)], qrecv.at[t],
+    def q_copy(u):
+        return pltpu.make_async_remote_copy(
+            bx.at[half_rows(u), :], bq.at[half_rows(u), :], qsend.at[lax.rem(u, XD)], qrecv.at[u],
+            device_id=p_to, device_id_type=MESH,
+        )
+
+    def q_direct(u):
+        rows = pl.ds(pl.multiple_of(place(far) * KC + lax.rem(u, 2) * HALF, HALF), HALF)
+        return pltpu.make_async_remote_copy(
+            bx.at[half_rows(u), :], bbuf.at[last_slot, rows, :], qsend.at[lax.rem(u, XD)], qrecv.at[u],
             device_id=p_to, device_id_type=MESH,
         )
 
     def place(k):
         return jnp.where(k // 2 == y, lax.rem(k, 2), 2 + jnp.where(lax.rem(k, 2) == z, 0, 1))
 
-    def a_loads(s):
+    def a_loads(s, parts=range(4)):
         slot = lax.rem(s // Q, 2)
         sources = [a_piece(s, 0), a_piece(s, 1), ay.at[s // Q, a_rows(s), :], az.at[s // Q, a_rows(s), :]]
         return [
             pltpu.make_async_copy(
-                src, abuf.at[slot, a_rows(s), pl.ds(p * KC, KC)], asem.at[lax.rem(s, AHEAD + Q), p]
+                sources[p], abuf.at[slot, a_rows(s), pl.ds(p * KC, KC)], asem.at[lax.rem(s, AHEAD + Q), p]
             )
-            for p, src in enumerate(sources)
+            for p in parts
         ]
 
-    def b_loads(t):
+    def b_loads(t, parts=range(4)):
         slot = lax.rem(t, 2)
         sources = [
             (b_piece(t), i),
@@ -99,9 +127,11 @@
         ]
         return [
             pltpu.make_async_copy(
-                src, bbuf.at[slot, pl.ds(pl.multiple_of(place(k) * KC, KC), KC), :], bsem.at[slot, n]
+                sources[n][0],
+                bbuf.at[slot, pl.ds(pl.multiple_of(place(sources[n][1]) * KC, KC), KC), :],
+                bsem.at[slot, n],
             )
-            for n, (src, k) in enumerate(sources)
+            for n in parts
         ]
 
     def compute(s):
@@ -119,8 +149,9 @@
 
     for s in range(YD):
         y_copy(s).start()
-    for t in range(XD):
-        x_copy(t).start()
+    for u in range(XD):
+        x_copy(u).start()
+    for t in range(PD):
         p_copy(t).start()
 
     @pl.loop(0, m // 128)
@@ -144,66 +175,120 @@
         for ld in a_loads(s):
             ld.start()
 
-    @pl.loop(0, ticks + WORK - Q)
+    @pl.loop(0, ticks)
     def _(s):
         r, q = s // Q, lax.rem(s, Q)
 
-        @pl.when(s < ticks)
-        def _():
-            @pl.when(s >= ZD)
-            def _():
-                z_copy(s - ZD).wait_send()
-
-            y_copy(s).wait_recv()
+        @pl.when(s >= ZD)
+        def _():
+            z_copy(s - ZD).wait_send()
+
+        y_copy(s).wait_recv()
+
+        @pl.when(s < ticks - 2)
+        def _():
             z_copy(s).start()
-            y_copy(s).wait_send()
-
-            @pl.when(s + YD < ticks)
-            def _():
-                y_copy(s + YD).start()
-
-            @pl.when(q == Q - 1)
-            def _():
-                @pl.when(r >= XD)
-                def _():
-                    q_copy(r - XD).wait_send()
-
-                x_copy(r).wait_recv()
-                q_copy(r).start()
-                x_copy(r).wait_send()
-                p_copy(r).wait_send()
-
-                @pl.when(r + XD < rounds)
-                def _():
-                    x_copy(r + XD).start()
-                    p_copy(r + XD).start()
-
-        @pl.when((q == 1) & (r >= 1))
+
+        @pl.when(s == ticks - 2)
+        def _():
+            pl.semaphore_wait(zfree, 1)
+            z_direct(s).start()
+
+        y_copy(s).wait_send()
+
+        @pl.when(s + YD < ticks)
+        def _():
+            y_copy(s + YD).start()
+
+        @pl.when(s == ticks - 3)
+        def _():
+            pl.semaphore_wait(yfree, 1)
+            w_copy().start()
+
+        @pl.when(lax.rem(q, Q // 2) == Q // 2 - 1)
+        def _():
+            u = s // (Q // 2)
+
+            @pl.when(u >= XD)
+            def _():
+                q_copy(u - XD).wait_send()
+
+            x_copy(u).wait_recv()
+
+            @pl.when(u < halves - 2)
+            def _():
+                q_copy(u).start()
+
+            @pl.when(u == halves - 2)
+            def _():
+                pl.semaphore_wait(pfree, 1)
+
+            @pl.when(u >= halves - 2)
+            def _():
+                q_direct(u).start()
+
+            x_copy(u).wait_send()
+
+            @pl.when(u + XD < halves)
+            def _():
+                x_copy(u + XD).start()
+
+        @pl.when(q == Q - 1)
+        def _():
+            p_copy(r).wait_send()
+
+            @pl.when(r + PD < rounds)
+            def _():
+                p_copy(r + PD).start()
+
+        @pl.when(s >= LOAD)
+        def _():
+            load(s - LOAD)
+
+        @pl.when(s >= WORK)
+        def _():
+            work(s - WORK)
+
+        @pl.when((q == 0) & (r >= 1))
         def _():
             p_copy(r - 1).wait_recv()
-            q_copy(r - 1).wait_recv()
+            q_copy(2 * r - 2).wait_recv()
+            q_copy(2 * r - 1).wait_recv()
             for ld in b_loads(r - 1):
                 ld.start()
 
-        @pl.when((s >= LOAD) & (s - LOAD < ticks))
-        def _():
-            load(s - LOAD)
-
-        @pl.when(s >= WORK)
-        def _():
-            work(s - WORK)
-
-    for s in range(ticks + WORK - Q - LOAD, ticks):
-        load(s)
-    for s in range(ticks - ZD, ticks):
+        @pl.when(s == ticks - Q)
+        def _():
+            for free, to in ((yfree, y_to), (zfree, z_to), (pfree, p_to)):
+                pl.semaphore_signal(free, inc=1, device_id=to, device_id_type=MESH)
+
+    load(ticks - 4)
+    for s in range(ticks - 3, ticks):
+        for ld in a_loads(s, range(3)):
+            ld.start()
+    p_copy(rounds - 1).wait_recv()
+    for ld in b_loads(rounds - 1, range(3)):
+        ld.start()
+    work(ticks - WORK)
+    z_copy(ticks - 3).wait_recv()
+    a_loads(ticks - 3, [3])[0].start()
+    for s in range(ticks - ZD, ticks - 1):
         z_copy(s).wait_send()
-    for t in range(rounds - XD, rounds):
-        q_copy(t).wait_send()
-    for s in range(ticks - Q, ticks):
+    w_copy().wait_send()
+    for u in range(halves - XD, halves):
+        q_copy(u).wait_send()
+    for s in range(ticks - Q, ticks - 2):
         for ld in a_loads(s):
             ld.wait()
-    for ld in b_loads(rounds - 1):
+    for s in range(ticks - 2, ticks):
+        for ld in a_loads(s, range(3)):
+            ld.wait()
+    for ld in b_loads(rounds - 1, range(3)):
         ld.wait()
+    for u in range(halves - 2, halves):
+        q_copy(u).wait_recv()
+    for s in range(ticks - 2, ticks):
+        z_copy(s).wait_recv()
 
 
 def finish_kernel(slot, c_ref, abuf, bbuf, out, total, sem):
@@ -254,8 +339,9 @@
             in_specs=[any_spec] * 2,
             out_specs=(vmem_spec,) * 3 + (any_spec,) * 5,
             scratch_shapes=[
-                dma((YD,)), dma((ticks,)), dma((ZD,)), dma((ticks,)), dma((XD,)), dma((rounds,)),
-                dma((XD,)), dma((rounds,)), dma((XD,)), dma((rounds,)), dma((AHEAD + Q, 4)), dma((2, 4)),
+                dma((YD,)), dma((ticks,)), dma((ZD,)), dma((ticks,)), dma, dma((XD,)), dma((2 * rounds,)),
+                dma((PD,)), dma((rounds,)), dma((XD,)), dma((2 * rounds,)), dma((AHEAD + Q, 4)), dma((2, 4)),
+                *[pltpu.SemaphoreType.REGULAR] * 3,
             ],
             compiler_params=pltpu.CompilerParams(
                 collective_id=0, has_side_effects=True, vmem_limit_bytes=4 * 2**20

time: 435 us -> 434 us (level)
  no operation moved by 1% of the time
where the time goes in v3:
time: 434 us
  Pallas kernels  434 us (100%)
    pallas_call x1, Pallas kernels, local_product(): pl.pallas_call(gather_kernel, name='gather', out_shape=(pltpu.VMEM((m, m)...  420 us
    pallas_call x1, Pallas kernels, local_product(): pl.pallas_call(functools.partial(finish_kernel, (rounds - 1) % 2), name='...  14.1 us

profile of v3, /device:TPU:0, one launch (start us, length us, event | category | flops | bytes accessed | tf_op | source)
XLA Modules:
  0.0 434.0 jit_solution(1668000562012141211)
XLA Ops:
  0.0 419.8 %gather.1 = (f32[3072,3072]{1,0:T(8,128)S(1)}, bf16[2,3072,512]{2,1,0:T(8,128)(2,1)S(1)}, bf16[2,512,3072]{2,1,0:T(8,128)(2,1)S(1)}, bf16[24,3072,128]{2,1,0:T(8...) custom-call(bf16[3072,6144]{1,0:T(8,128)(2,1)} %a_ref.1, ...), custom_call_target="tpu_custom_call" | custom-call | tf_op jit(solution)/shard_map/gather/pallas_call | solution.py:326
  419.9 14.1 %finish.1 = (f32[3072,3072]{1,0:T(8,128)}, f32[3072,3072]{1,0:T(8,128)S(1)}) custom-call(f32[3072,3072]{1,0:T(8,128)S(1)} %get-tuple-element.9.c_ref, bf16[2,3072,512]{2,1,0:T(8,128)(2,1)S(1)} %get-tuple-element.10.abuf, bf16[2,512,3072]{2,1,0:T(8,128)(2,1)S(1)} %get-tuple-element.11.bbuf), custom_call_target="tpu_custom_call", output_to_operand_aliasing={{1}: (0, {})} | custom-call | tf_op jit(solution)/shard_map/finish/pallas_call | solution.py:351

commit v4 on v3

--- a/solution.py
+++ b/solution.py
@@ -245,10 +245,6 @@
         def _():
             load(s - LOAD)
 
-        @pl.when(s >= WORK)
-        def _():
-            work(s - WORK)
-
         @pl.when((q == 0) & (r >= 1))
         def _():
             p_copy(r - 1).wait_recv()
@@ -256,6 +252,10 @@
             q_copy(2 * r - 1).wait_recv()
             for ld in b_loads(r - 1):
                 ld.start()
+
+        @pl.when(s >= WORK)
+        def _():
+            work(s - WORK)
 
         @pl.when(s == ticks - Q)
         def _():
@@ -296,21 +296,18 @@
     tm, tn = m // Q, m // NT
 
     def write(k, n):
-        at = pl.ds(pl.multiple_of(k * tm, tm), tm), pl.ds(n * tn, tn)
+        at = pl.ds(k * tm, tm), pl.ds(n * tn, tn)
         return pltpu.make_async_copy(total.at[at], out.at[at], sem.at[k, n])
 
-    @pl.loop(0, Q)
-    def _(k):
-        rows = pl.ds(pl.multiple_of(k * tm, tm), tm)
+    for k in range(Q):
+        rows = pl.ds(k * tm, tm)
         for n in range(NT):
             cols = pl.ds(n * tn, tn)
             total[rows, cols] = c_ref[rows, cols] + jnp.dot(
                 abuf[slot, rows, :], bbuf[slot, :, cols], preferred_element_type=jnp.float32
             )
             write(k, n).start()
-
-    @pl.loop(0, Q)
-    def _(k):
+    for k in range(Q):
         for n in range(NT):
             write(k, n).wait()
 

time: 434 us -> 434 us (level)
  no operation moved by 1% of the time
where the time goes in v4:
time: 434 us
  Pallas kernels  434 us (100%)
    pallas_call x1, Pallas kernels, local_product(): pl.pallas_call(gather_kernel, name='gather', out_shape=(pltpu.VMEM((m, m)...  420 us
    pallas_call x1, Pallas kernels, local_product(): pl.pallas_call(functools.partial(finish_kernel, (rounds - 1) % 2), name='...  14 us

profile of v4, /device:TPU:0, one launch (start us, length us, event | category | flops | bytes accessed | tf_op | source)
XLA Modules:
  0.0 433.8 jit_solution(16253726870970554927)
XLA Ops:
  0.0 419.8 %gather.1 = (f32[3072,3072]{1,0:T(8,128)S(1)}, bf16[2,3072,512]{2,1,0:T(8,128)(2,1)S(1)}, bf16[2,512,3072]{2,1,0:T(8,128)(2,1)S(1)}, bf16[24,3072,128]{2,1,0:T(8...) custom-call(bf16[3072,6144]{1,0:T(8,128)(2,1)} %a_ref.1, ...), custom_call_target="tpu_custom_call" | custom-call | tf_op jit(solution)/shard_map/gather/pallas_call | solution.py:323
  419.8 14.0 %finish.1 = (f32[3072,3072]{1,0:T(8,128)}, f32[3072,3072]{1,0:T(8,128)S(1)}) custom-call(f32[3072,3072]{1,0:T(8,128)S(1)} %get-tuple-element.9.c_ref, bf16[2,3072,512]{2,1,0:T(8,128)(2,1)S(1)} %get-tuple-element.10.abuf, bf16[2,512,3072]{2,1,0:T(8,128)(2,1)S(1)} %get-tuple-element.11.bbuf), custom_call_target="tpu_custom_call", output_to_operand_aliasing={{1}: (0, {})} | custom-call | tf_op jit(solution)/shard_map/finish/pallas_call | solution.py:348

commit v5 on v4

--- a/solution.py
+++ b/solution.py
@@ -21,6 +21,10 @@
 WORK = Q + 1
 
 
+def rem(a, b):
+    return a % b if isinstance(a, int) else lax.rem(a, b)
+
+
 def gather_kernel(
     a_ref, b_ref,
     c_ref, abuf, bbuf, ay, az, bx, bp, bq,
@@ -33,12 +37,12 @@
     ticks, halves = rounds * Q, 2 * rounds
     last_slot = (rounds - 1) % 2
     z_to, y_to = {"dep": 1 - z}, {"col": 1 - y}
-    swap = 1 - 2 * lax.rem(i, 2)
-    far = lax.rem(i + 2, 4)
+    swap = 1 - 2 * rem(i, 2)
+    far = rem(i + 2, 4)
     x_to, p_to = {"row": far}, {"row": i + swap}
 
     def a_rows(s):
-        return pl.ds(pl.multiple_of(lax.rem(s, Q) * mq, mq), mq)
+        return pl.ds(pl.multiple_of(rem(s, Q) * mq, mq), mq)
 
     def a_piece(s, h):
         return a_ref.at[a_rows(s), pl.ds(pl.multiple_of(h * m + s // Q * KC, KC), KC)]
@@ -51,20 +55,20 @@
 
     def y_copy(s):
         return pltpu.make_async_remote_copy(
-            a_piece(s, z), ay.at[s // Q, a_rows(s), :], ysend.at[lax.rem(s, YD)], yrecv.at[s],
+            a_piece(s, z), ay.at[s // Q, a_rows(s), :], ysend.at[rem(s, YD)], yrecv.at[s],
             device_id=y_to, device_id_type=MESH,
         )
 
     def z_copy(s):
         return pltpu.make_async_remote_copy(
-            ay.at[s // Q, a_rows(s), :], az.at[s // Q, a_rows(s), :], zsend.at[lax.rem(s, ZD)], zrecv.at[s],
+            ay.at[s // Q, a_rows(s), :], az.at[s // Q, a_rows(s), :], zsend.at[rem(s, ZD)], zrecv.at[s],
             device_id=z_to, device_id_type=MESH,
         )
 
     def z_direct(s):
         return pltpu.make_async_remote_copy(
             ay.at[s // Q, a_rows(s), :], abuf.at[last_slot, a_rows(s), pl.ds(3 * KC, KC)],
-            zsend.at[lax.rem(s, ZD)], zrecv.at[s],
+            zsend.at[rem(s, ZD)], zrecv.at[s],
             device_id=z_to, device_id_type=MESH,
         )
 
@@ -81,44 +85,44 @@
     def x_copy(u):
         return pltpu.make_async_remote_copy(
             b_ref.at[half_rows(u), pl.ds(pl.multiple_of(z * m, m), m)], bx.at[half_rows(u), :],
-            xsend.at[lax.rem(u, XD)], xrecv.at[u],
+            xsend.at[rem(u, XD)], xrecv.at[u],
             device_id=x_to, device_id_type=MESH,
         )
 
     def p_copy(t):
         return pltpu.make_async_remote_copy(
-            b_piece(t), bp.at[b_rows(t), :], psend.at[lax.rem(t, PD)], precv.at[t],
+            b_piece(t), bp.at[b_rows(t), :], psend.at[rem(t, PD)], precv.at[t],
             device_id=p_to, device_id_type=MESH,
         )
 
     def q_copy(u):
         return pltpu.make_async_remote_copy(
-            bx.at[half_rows(u), :], bq.at[half_rows(u), :], qsend.at[lax.rem(u, XD)], qrecv.at[u],
+            bx.at[half_rows(u), :], bq.at[half_rows(u), :], qsend.at[rem(u, XD)], qrecv.at[u],
             device_id=p_to, device_id_type=MESH,
         )
 
     def q_direct(u):
-        rows = pl.ds(pl.multiple_of(place(far) * KC + lax.rem(u, 2) * HALF, HALF), HALF)
-        return pltpu.make_async_remote_copy(
-            bx.at[half_rows(u), :], bbuf.at[last_slot, rows, :], qsend.at[lax.rem(u, XD)], qrecv.at[u],
+        rows = pl.ds(pl.multiple_of(place(far) * KC + rem(u, 2) * HALF, HALF), HALF)
+        return pltpu.make_async_remote_copy(
+            bx.at[half_rows(u), :], bbuf.at[last_slot, rows, :], qsend.at[rem(u, XD)], qrecv.at[u],
             device_id=p_to, device_id_type=MESH,
         )
 
     def place(k):
-        return jnp.where(k // 2 == y, lax.rem(k, 2), 2 + jnp.where(lax.rem(k, 2) == z, 0, 1))
+        return jnp.where(k // 2 == y, rem(k, 2), 2 + jnp.where(rem(k, 2) == z, 0, 1))
 
     def a_loads(s, parts=range(4)):
-        slot = lax.rem(s // Q, 2)
+        slot = rem(s // Q, 2)
         sources = [a_piece(s, 0), a_piece(s, 1), ay.at[s // Q, a_rows(s), :], az.at[s // Q, a_rows(s), :]]
         return [
             pltpu.make_async_copy(
-                sources[p], abuf.at[slot, a_rows(s), pl.ds(p * KC, KC)], asem.at[lax.rem(s, AHEAD + Q), p]
+                sources[p], abuf.at[slot, a_rows(s), pl.ds(p * KC, KC)], asem.at[rem(s, AHEAD + Q), p]
             )
             for p in parts
         ]
 
     def b_loads(t, parts=range(4)):
-        slot = lax.rem(t, 2)
+        slot = rem(t, 2)
         sources = [
             (b_piece(t), i),
             (bp.at[b_rows(t), :], i + swap),
@@ -134,13 +138,11 @@
             for n in parts
         ]
 
-    def compute(s):
-        slot, rows = lax.rem(s // Q, 2), a_rows(s)
-        for n in range(NT):
-            cols = pl.ds(n * tn, tn)
-            c_ref[rows, cols] += jnp.dot(
-                abuf[slot, rows, :], bbuf[slot, :, cols], preferred_element_type=jnp.float32
-            )
+    def tile(s, n):
+        slot, rows, cols = rem(s // Q, 2), a_rows(s), pl.ds(n * tn, tn)
+        c_ref[rows, cols] += jnp.dot(
+            abuf[slot, rows, :], bbuf[slot, :, cols], preferred_element_type=jnp.float32
+        )
 
     barrier = pltpu.get_barrier_semaphore()
     for to in (z_to, y_to, x_to, p_to):
@@ -159,25 +161,22 @@
         rows = pl.ds(pl.multiple_of(n * 128, 128), 128)
         c_ref[rows, :] = jnp.zeros((128, m), jnp.float32)
 
-    def work(s):
+    def ready(s):
         for ld in a_loads(s):
             ld.wait()
 
-        @pl.when(lax.rem(s, Q) == 0)
+        @pl.when(rem(s, Q) == 0)
         def _():
             for ld in b_loads(s // Q):
                 ld.wait()
-
-        compute(s)
 
     def load(s):
         z_copy(s).wait_recv()
         for ld in a_loads(s):
             ld.start()
 
-    @pl.loop(0, ticks)
-    def _(s):
-        r, q = s // Q, lax.rem(s, Q)
+    def tick(s):
+        r, q = s // Q, rem(s, Q)
 
         @pl.when(s >= ZD)
         def _():
@@ -205,7 +204,7 @@
             pl.semaphore_wait(yfree, 1)
             w_copy().start()
 
-        @pl.when(lax.rem(q, Q // 2) == Q // 2 - 1)
+        @pl.when(rem(q, Q // 2) == Q // 2 - 1)
         def _():
             u = s // (Q // 2)
 
@@ -253,23 +252,40 @@
             for ld in b_loads(r - 1):
                 ld.start()
 
+    @pl.loop(0, ticks - Q + 1)
+    def _(s):
+        tick(s)
+
         @pl.when(s >= WORK)
         def _():
-            work(s - WORK)
+            ready(s - WORK)
+            for n in range(NT):
+                tile(s - WORK, n)
 
         @pl.when(s == ticks - Q)
         def _():
             for free, to in ((yfree, y_to), (zfree, z_to), (pfree, p_to)):
                 pl.semaphore_signal(free, inc=1, device_id=to, device_id_type=MESH)
 
-    load(ticks - 4)
-    for s in range(ticks - 3, ticks):
-        for ld in a_loads(s, range(3)):
-            ld.start()
-    p_copy(rounds - 1).wait_recv()
-    for ld in b_loads(rounds - 1, range(3)):
-        ld.start()
-    work(ticks - WORK)
+    tiles = [(s, n) for s in range(ticks - 2 * Q, ticks - Q) for n in range(NT)]
+    share = -(-len(tiles) // (Q - 1))
+    for k in range(Q - 1):
+        tick(ticks - Q + 1 + k)
+        if k == 0:
+            p_copy(rounds - 1).wait_recv()
+            for ld in b_loads(rounds - 1, range(2)):
+                ld.start()
+        if k == Q - 2:
+            load(ticks - 4)
+            for s in range(ticks - 3, ticks):
+                for ld in a_loads(s, range(3)):
+                    ld.start()
+            b_loads(rounds - 1, [2])[0].start()
+        for s, n in tiles[k * share : (k + 1) * share]:
+            if n == 0:
+                ready(s)
+            tile(s, n)
+
     z_copy(ticks - 3).wait_recv()
     a_loads(ticks - 3, [3])[0].start()
     for s in range(ticks - ZD, ticks - 1):
@@ -294,22 +310,20 @@
 def finish_kernel(slot, c_ref, abuf, bbuf, out, total, sem):
     m = c_ref.shape[0]
     tm, tn = m // Q, m // NT
-
-    def write(k, n):
-        at = pl.ds(k * tm, tm), pl.ds(n * tn, tn)
-        return pltpu.make_async_copy(total.at[at], out.at[at], sem.at[k, n])
-
-    for k in range(Q):
-        rows = pl.ds(k * tm, tm)
+    ends = [tm // 4, tm // 4, tm // 2]
+    writes, top = [], 0
+    for k, height in enumerate(ends + [tm] * (Q - 2) + ends[::-1]):
+        rows = pl.ds(top, height)
+        top += height
         for n in range(NT):
             cols = pl.ds(n * tn, tn)
             total[rows, cols] = c_ref[rows, cols] + jnp.dot(
                 abuf[slot, rows, :], bbuf[slot, :, cols], preferred_element_type=jnp.float32
             )
-            write(k, n).start()
-    for k in range(Q):
-        for n in range(NT):
-            write(k, n).wait()
+            writes.append(pltpu.make_async_copy(total.at[rows, cols], out.at[rows, cols], sem.at[k, n]))
+            writes[-1].start()
+    for write in writes:
+        write.wait()
 
 
 def solution(mesh):
@@ -352,7 +366,7 @@
             in_specs=[vmem_spec] * 3,
             out_specs=(any_spec, vmem_spec),
             input_output_aliases={0: 1},
-            scratch_shapes=[dma((Q, NT))],
+            scratch_shapes=[dma((Q + 4, NT))],
             compiler_params=pltpu.CompilerParams(vmem_limit_bytes=4 * 2**20),
         )(c, abuf, bbuf)[0]
 

time: 434 us -> 432 us (level)
  no operation moved by 1% of the time
where the time goes in v5:
time: 432 us
  Pallas kernels  432 us (100%)
    pallas_call x1, Pallas kernels, local_product(): pl.pallas_call(gather_kernel, name='gather', out_shape=(pltpu.VMEM((m, m)...  417 us
    pallas_call x1, Pallas kernels, local_product(): pl.pallas_call(functools.partial(finish_kernel, (rounds - 1) % 2), name='...  14.5 us

profile of v5, /device:TPU:0, one launch (start us, length us, event | category | flops | bytes accessed | tf_op | source)
XLA Modules:
  0.0 432.2 jit_solution(5543094195231295136)
XLA Ops:
  0.0 417.5 %gather.1 = (f32[3072,3072]{1,0:T(8,128)S(1)}, bf16[2,3072,512]{2,1,0:T(8,128)(2,1)S(1)}, bf16[2,512,3072]{2,1,0:T(8,128)(2,1)S(1)}, bf16[24,3072,128]{2,1,0:T(8...) custom-call(bf16[3072,6144]{1,0:T(8,128)(2,1)} %a_ref.1, ...), custom_call_target="tpu_custom_call" | custom-call | tf_op jit(solution)/shard_map/gather/pallas_call | solution.py:337
  417.5 14.5 %finish.1 = (f32[3072,3072]{1,0:T(8,128)}, f32[3072,3072]{1,0:T(8,128)S(1)}) custom-call(f32[3072,3072]{1,0:T(8,128)S(1)} %get-tuple-element.9.c_ref, bf16[2,3072,512]{2,1,0:T(8,128)(2,1)S(1)} %get-tuple-element.10.abuf, bf16[2,512,3072]{2,1,0:T(8,128)(2,1)S(1)} %get-tuple-element.11.bbuf), custom_call_target="tpu_custom_call", output_to_operand_aliasing={{1}: (0, {})} | custom-call | tf_op jit(solution)/shard_map/finish/pallas_call | solution.py:362

commit v6 on v5

--- a/solution.py
+++ b/solution.py
@@ -310,11 +310,9 @@
 def finish_kernel(slot, c_ref, abuf, bbuf, out, total, sem):
     m = c_ref.shape[0]
     tm, tn = m // Q, m // NT
-    ends = [tm // 4, tm // 4, tm // 2]
-    writes, top = [], 0
-    for k, height in enumerate(ends + [tm] * (Q - 2) + ends[::-1]):
-        rows = pl.ds(top, height)
-        top += height
+    writes = []
+    for k in range(Q):
+        rows = pl.ds(k * tm, tm)
         for n in range(NT):
             cols = pl.ds(n * tn, tn)
             total[rows, cols] = c_ref[rows, cols] + jnp.dot(
@@ -366,7 +364,7 @@
             in_specs=[vmem_spec] * 3,
             out_specs=(any_spec, vmem_spec),
             input_output_aliases={0: 1},
-            scratch_shapes=[dma((Q + 4, NT))],
+            scratch_shapes=[dma((Q, NT))],
             compiler_params=pltpu.CompilerParams(vmem_limit_bytes=4 * 2**20),
         )(c, abuf, bbuf)[0]
 

time: 432 us -> 432 us (level)
  no operation moved by 1% of the time
where the time goes in v6:
time: 432 us
  Pallas kernels  432 us (100%)
    pallas_call x1, Pallas kernels, local_product(): pl.pallas_call(gather_kernel, name='gather', out_shape=(pltpu.VMEM((m, m)...  417 us
    pallas_call x1, Pallas kernels, local_product(): pl.pallas_call(functools.partial(finish_kernel, (rounds - 1) % 2), name='...  14.2 us

profile of v6, /device:TPU:0, one launch (start us, length us, event | category | flops | bytes accessed | tf_op | source)
XLA Modules:
  0.0 431.8 jit_solution(16938600675146859607)
XLA Ops:
  0.0 417.5 %gather.1 = (f32[3072,3072]{1,0:T(8,128)S(1)}, bf16[2,3072,512]{2,1,0:T(8,128)(2,1)S(1)}, bf16[2,512,3072]{2,1,0:T(8,128)(2,1)S(1)}, bf16[24,3072,128]{2,1,0:T(8...) custom-call(bf16[3072,6144]{1,0:T(8,128)(2,1)} %a_ref.1, ...), custom_call_target="tpu_custom_call" | custom-call | tf_op jit(solution)/shard_map/gather/pallas_call | solution.py:335
  417.5 14.2 %finish.1 = (f32[3072,3072]{1,0:T(8,128)}, f32[3072,3072]{1,0:T(8,128)S(1)}) custom-call(f32[3072,3072]{1,0:T(8,128)S(1)} %get-tuple-element.9.c_ref, bf16[2,3072,512]{2,1,0:T(8,128)(2,1)S(1)} %get-tuple-element.10.abuf, bf16[2,512,3072]{2,1,0:T(8,128)(2,1)S(1)} %get-tuple-element.11.bbuf), custom_call_target="tpu_custom_call", output_to_operand_aliasing={{1}: (0, {})} | custom-call | tf_op jit(solution)/shard_map/finish/pallas_call | solution.py:360
